TPU v7x, 32 devices: a whole 2x2x4 slice. The times are simulated.
32 devices in a mesh: gx: 4 (over y, x), gy: 4 (over z), gz: 2 (over core).
Axes of the slice: x: 2, y: 2, z: 4, core: 2. Of those that a mesh axis runs over, the one named last changes fastest.
Arguments:
- residual: float32 [2, 128, 128, 1024], P(None, 'gx', 'gy', 'gz'), may hold values from -6 to 6
- eig_x: float32 [4, 48, 48], P('gx'), may hold values from -0.875 to 0.875
- eig_y: float32 [4, 48, 48], P('gy'), may hold values from -0.875 to 0.875
- eig_z: float32 [2, 528, 528], P('gz'), may hold values from -0.25 to 0.25
- lam_x: float32 [4, 48], P('gx'), may hold values from 0.5 to 4
- lam_y: float32 [4, 48], P('gy'), may hold values from 0.5 to 4
- lam_z: float32 [2, 528], P('gz'), may hold values from 0.5 to 4
- basis_x: float32 [4, 4, 32], P('gx'), may hold values from -2.1 to 2.1
- basis_y: float32 [4, 4, 32], P('gy'), may hold values from -2.1 to 2.1
- basis_z: float32 [2, 4, 512], P('gz'), may hold values from -2.1 to 2.1
- coarse_inverse: float32 [2048, 2048], P(('gx', 'gy', 'gz')), may hold values from -0.0064086914 to 0.0064086914
Outputs:
- precond: float32 [2, 128, 128, 1024], P(None, 'gx', 'gy', 'gz')
All inputs are finite; a program needn't handle non-finite values.
Results may differ from a plain program's by a relative error of at most 0.0003.
Values sent between devices are 32-bit elements; how exact they have to be, the bound alone decides.
A program may use at most 128 MiB of HBM per device.

v0:
```python
import functools

import jax
import jax.numpy as jnp
from jax import lax
from jax.experimental import pallas as pl
from jax.experimental.pallas import tpu as pltpu
from jax.sharding import PartitionSpec as P

NODES = 8
LANES = 128
HIGH = lax.Precision.HIGHEST
BF = jnp.bfloat16
F32 = jnp.float32


def split_host(x):
    hi = lax.reduce_precision(x, 8, 7)
    return hi.astype(BF), lax.reduce_precision(x - hi, 8, 7).astype(BF)


def split(x):
    hi = x.astype(BF)
    return hi, (x - hi.astype(F32)).astype(BF)


def halo_kernel(
    sizes, res, bz, kron, ext, every, zeros, part, own_sem, zero_sem, sx, rx, sy, ry, sc, rc, sg, rg
):
    n_gx, n_gy, n_gz = sizes
    own_x, own_y = res.shape[1], res.shape[2]
    w = NODES
    gx = lax.axis_index("gx")
    gy = lax.axis_index("gy")
    has_x = (gx > 0, gx < n_gx - 1)
    has_y = (gy > 0, gy < n_gy - 1)
    to_x = (gx - 1, gx + 1)
    to_y = (gy - 1, gy + 1)
    gz = lax.axis_index("gz")
    place = {"gx": gx, "gy": gy, "gz": gz}
    barrier = pltpu.get_barrier_semaphore()
    peers = [
        {axis: lax.rem(place[axis] + step, count)}
        for axis, count in zip(("gz", "gy", "gx"), (n_gz, n_gy, n_gx))
        for step in range(1, count)
    ]
    for peer in peers:
        pl.semaphore_signal(barrier, inc=1, device_id=peer)
    pl.semaphore_wait(barrier, len(peers))

    src = lambda side, own: pl.ds(0, w) if side == 0 else pl.ds(own - w, w)
    dst = lambda side, own: pl.ds(own + w, w) if side == 0 else pl.ds(0, w)
    mine = lambda side, own: pl.ds(0, w) if side == 0 else pl.ds(own + w, w)
    chunks = ((0, w), (own_y - w, w), (w, own_y - 2 * w))

    def send_x(side, c):
        start, size = chunks[c]
        return pltpu.make_async_remote_copy(
            src_ref=res.at[:, src(side, own_x), pl.ds(start, size)],
            dst_ref=ext.at[:, dst(side, own_x), pl.ds(w + start, size)],
            send_sem=sx.at[side, c],
            recv_sem=rx.at[side, c],
            device_id={"gx": to_x[side]},
        )

    def get_x(side, c):
        start, size = chunks[c]
        return pltpu.make_async_remote_copy(
            src_ref=res.at[:, src(1 - side, own_x), pl.ds(start, size)],
            dst_ref=ext.at[:, mine(side, own_x), pl.ds(w + start, size)],
            send_sem=sx.at[1 - side, c],
            recv_sem=rx.at[1 - side, c],
            device_id={"gx": to_x[side]},
        )

    def send_y(side):
        return pltpu.make_async_remote_copy(
            src_ref=res.at[:, :, src(side, own_y)],
            dst_ref=ext.at[:, pl.ds(w, own_x), dst(side, own_y)],
            send_sem=sy.at[side],
            recv_sem=ry.at[side],
            device_id={"gy": to_y[side]},
        )

    def get_y(side):
        return pltpu.make_async_remote_copy(
            src_ref=res.at[:, :, src(1 - side, own_y)],
            dst_ref=ext.at[:, pl.ds(w, own_x), mine(side, own_y)],
            send_sem=sy.at[1 - side],
            recv_sem=ry.at[1 - side],
            device_id={"gy": to_y[side]},
        )

    def send_c(a, b):
        rows = pl.ds(w, w) if b == 0 else pl.ds(own_y, w)
        return pltpu.make_async_remote_copy(
            src_ref=ext.at[:, mine(a, own_x), rows],
            dst_ref=ext.at[:, mine(a, own_x), dst(b, own_y)],
            send_sem=sc.at[a, b],
            recv_sem=rc.at[a, b],
            device_id={"gy": to_y[b]},
        )

    def get_c(a, b):
        return pltpu.make_async_remote_copy(
            src_ref=ext.at[:, mine(a, own_x), pl.ds(w, w)],
            dst_ref=ext.at[:, mine(a, own_x), mine(b, own_y)],
            send_sem=sc.at[a, 1 - b],
            recv_sem=rc.at[a, 1 - b],
            device_id={"gy": to_y[b]},
        )

    for c in range(3):
        for side in range(2):
            @pl.when(has_x[side])
            def _():
                send_x(side, c).start()

    own = pltpu.make_async_copy(
        res, ext.at[:, pl.ds(w, own_x), pl.ds(w, own_y)], own_sem
    )
    own.start()
    zeros[...] = jnp.zeros_like(zeros)

    nv, mz = res.shape[0], res.shape[3]
    rows, lanes = part.shape[1], part.shape[2]
    step = 4

    @pl.loop(0, nv * (own_x // step))
    def _(i):
        v = i // (own_x // step)
        a = lax.rem(i, own_x // step)
        hi, lo = split(res[v, pl.ds(a * step, step)].reshape(step * own_y, mz))
        both = dot(hi, bz[...])
        both = both[:, :lanes] + both[:, lanes:] + dot(lo, bz[:, :lanes])
        part[v, pl.ds(pl.multiple_of(a * (step * own_y), 8), step * own_y), :] = both

    pairs = kron.shape[0]
    funcs = lanes // (nv * pairs)
    lane = lax.broadcasted_iota(jnp.int32, (pairs, lanes), 1)
    row = lax.broadcasted_iota(jnp.int32, (pairs, lanes), 0)
    total = jnp.zeros((1, lanes), F32)
    for v in range(nv):
        full = dot(kron[...], stack3(part[v]))
        keep = lane - row * funcs - v * (pairs * funcs)
        keep = jnp.logical_and(keep >= 0, keep < funcs)
        total += jnp.sum(jnp.where(keep, full, 0.0), axis=0, keepdims=True)
    every[gx, gy, gz] = total

    def stage(level):
        axis, count = (("gz", n_gz), ("gy", n_gy), ("gx", n_gx))[level]
        at = (every.at[gx, gy, gz], every.at[gx, gy], every.at[gx])[level]
        return [
            pltpu.make_async_remote_copy(
                src_ref=at, dst_ref=at, send_sem=sg.at[level, k - 1], recv_sem=rg.at[level, k - 1],
                device_id={axis: lax.rem(place[axis] + k, count)})
            for k in range(1, count)
        ]

    def arrived(level):
        axis, count = (("gz", n_gz), ("gy", n_gy), ("gx", n_gx))[level]
        for k in range(1, count):
            who = lax.rem(place[axis] + count - k, count)
            at = (every.at[gx, gy, who], every.at[gx, who], every.at[who])[level]
            pltpu.make_async_remote_copy(
                src_ref=at, dst_ref=at, send_sem=sg.at[level, k - 1], recv_sem=rg.at[level, k - 1],
                device_id={axis: who}).wait_recv()

    for copy in stage(0):
        copy.start()
    arrived(0)
    for copy in stage(1):
        copy.start()
    for side in range(2):
        @pl.when(has_y[side])
        def _():
            send_y(side).start()
    arrived(1)
    for copy in stage(2):
        copy.start()

    def zero_x(side):
        return pltpu.make_async_copy(
            zeros.at[:, pl.ds(0, w)],
            ext.at[:, mine(side, own_x), pl.ds(w, own_y)], zero_sem.at[side])

    def zero_y(side):
        return pltpu.make_async_copy(
            zeros.at[:, pl.ds(0, own_x), pl.ds(0, w)],
            ext.at[:, pl.ds(w, own_x), mine(side, own_y)], zero_sem.at[2 + side])

    def zero_c(a, b):
        return pltpu.make_async_copy(
            zeros.at[:, pl.ds(0, w), pl.ds(0, w)],
            ext.at[:, mine(a, own_x), mine(b, own_y)], zero_sem.at[4 + 2 * a + b])

    both = lambda a, b: jnp.logical_and(has_x[a], has_y[b])
    for s in range(2):
        pl.when(jnp.logical_not(has_x[s]))(lambda: zero_x(s).start())
        pl.when(jnp.logical_not(has_y[s]))(lambda: zero_y(s).start())
        for b in range(2):
            pl.when(jnp.logical_not(both(s, b)))(lambda: zero_c(s, b).start())

    for c in range(2):
        for a in range(2):
            @pl.when(has_x[a])
            def _():
                get_x(a, c).wait_recv()

            @pl.when(both(a, c))
            def _():
                send_c(a, c).start()
    for a in range(2):
        pl.when(has_x[a])(lambda: get_x(a, 2).wait_recv())
        pl.when(has_y[a])(lambda: get_y(a).wait_recv())
        for b in range(2):
            pl.when(both(a, b))(lambda: get_c(a, b).wait_recv())
    arrived(2)
    for level in range(3):
        for copy in stage(level):
            copy.wait_send()
    own.wait()
    for s in range(2):
        pl.when(jnp.logical_not(has_x[s]))(lambda: zero_x(s).wait())
        pl.when(jnp.logical_not(has_y[s]))(lambda: zero_y(s).wait())
        for b in range(2):
            pl.when(jnp.logical_not(both(s, b)))(lambda: zero_c(s, b).wait())
            pl.when(both(s, b))(lambda: send_c(s, b).wait_send())
        for c in range(3):
            pl.when(has_x[s])(lambda: send_x(s, c).wait_send())
        pl.when(has_y[s])(lambda: send_y(s).wait_send())


def extend(residual, bz, kron):
    sizes = tuple(lax.axis_size(axis) for axis in ("gx", "gy", "gz"))
    lanes = bz.shape[1] // 2
    peers = max(max(sizes) - 1, 1)
    nv, mx, my, mz = residual.shape
    w = NODES
    return pl.pallas_call(
        functools.partial(halo_kernel, sizes),
        out_shape=(
            jax.ShapeDtypeStruct((nv, mx + 2 * w, my + 2 * w, mz), F32),
            jax.ShapeDtypeStruct(sizes + (1, lanes), F32),
        ),
        in_specs=[pl.BlockSpec(memory_space=pltpu.VMEM)] * 3,
        out_specs=(
            pl.BlockSpec(memory_space=pltpu.HBM),
            pl.BlockSpec(memory_space=pltpu.VMEM),
        ),
        scratch_shapes=[
            pltpu.VMEM((nv, max(w, mx), my, mz), F32),
            pltpu.VMEM((nv, mx * my, lanes), F32),
            pltpu.SemaphoreType.DMA,
            pltpu.SemaphoreType.DMA((8,)),
            pltpu.SemaphoreType.DMA((2, 3)),
            pltpu.SemaphoreType.DMA((2, 3)),
            pltpu.SemaphoreType.DMA((2,)),
            pltpu.SemaphoreType.DMA((2,)),
            pltpu.SemaphoreType.DMA((2, 2)),
            pltpu.SemaphoreType.DMA((2, 2)),
            pltpu.SemaphoreType.DMA((3, peers)),
            pltpu.SemaphoreType.DMA((3, peers)),
        ],
        compiler_params=pltpu.CompilerParams(
            collective_id=0, has_side_effects=True, vmem_limit_bytes=32 * 2**20),
        name="halo",
    )(residual, bz, kron)


def stack3(x):
    hi, lo = split(x)
    return jnp.concatenate([hi, lo, hi], axis=0)


def dot(a, b):
    return jnp.dot(a, b, preferred_element_type=F32)


def load_rows(refs, start, size, stride):
    return jnp.concatenate([ref[pl.ds(start, size, stride), :] for ref in refs], axis=1)


def store_rows(refs, start, size, value):
    for i, ref in enumerate(refs):
        ref[pl.ds(pl.multiple_of(start, 8), size), :] = value[:, i * LANES : (i + 1) * LANES]


def forward_kernel(kx, ky, left, right, ex, ey, out, *tmp):
    ext = (left.at[0], right.at[0])

    @pl.loop(0, ky, unroll=8)
    def _(y):
        part = dot(ex[...], stack3(load_rows(ext, y, kx, ky)))
        store_rows(tmp, y * kx, kx, part)

    @pl.loop(0, kx, unroll=8)
    def _(p):
        part = dot(ey[...], stack3(load_rows(tmp, p, ky, kx)))
        out[0, pl.ds(pl.multiple_of(p * ky, 8), ky), :] = part


def forward_xy(ext, ex3, ey3, kx, ky):
    nv, rows, mz = ext.shape
    wide = 2 * LANES
    return pl.pallas_call(
        functools.partial(forward_kernel, kx, ky),
        grid=(nv, mz // wide),
        out_shape=jax.ShapeDtypeStruct(ext.shape, F32),
        in_specs=[
            pl.BlockSpec((1, rows, LANES), lambda v, z: (v, 0, 2 * z)),
            pl.BlockSpec((1, rows, LANES), lambda v, z: (v, 0, 2 * z + 1)),
            pl.BlockSpec(memory_space=pltpu.VMEM),
            pl.BlockSpec(memory_space=pltpu.VMEM),
        ],
        out_specs=pl.BlockSpec((1, rows, wide), lambda v, z: (v, 0, z)),
        scratch_shapes=[pltpu.VMEM((rows, LANES), F32)] * 2,
        compiler_params=pltpu.CompilerParams(vmem_limit_bytes=32 * 2**20),
        name="forward_xy",
    )(ext, ext, ex3, ey3)


def z_kernel(mz, t, low, high, lxy, lz, w1, w2, out):
    w = NODES
    lane = lax.broadcasted_iota(jnp.int32, low.shape, 1)
    edge = jnp.where(lane < w, high[...], jnp.where(lane >= LANES - w, low[...], 0.0))

    def pack(x):
        hi = x.astype(BF).astype(F32)
        lo = x - hi
        return (hi + pltpu.roll(lo, 2 * w, 1) + pltpu.roll(hi, 4 * w, 1)).astype(BF)

    hi, lo = split(t[...])
    spec = dot(jnp.concatenate([hi, lo, hi, pack(edge)], axis=1), w1[...])
    spec = spec / (lxy[:, :1] + lz[...])
    hi, lo = split(spec[:, :mz])
    out[...] = dot(jnp.concatenate([hi, lo, hi, pack(spec[:, mz:])], axis=1), w2[...])


def solve_z(t, low, high, lxy, lz, w1, w2):
    rows, mz = t.shape
    r = 288
    per = lxy.shape[0] // r
    row = lambda i: (i, 0)
    return pl.pallas_call(
        functools.partial(z_kernel, mz),
        grid=(rows // r,),
        out_shape=jax.ShapeDtypeStruct(t.shape, F32),
        in_specs=[
            pl.BlockSpec((r, mz), row),
            pl.BlockSpec((r, LANES), row),
            pl.BlockSpec((r, LANES), row),
            pl.BlockSpec((r, LANES), lambda i: (lax.rem(i, per), 0)),
            pl.BlockSpec(memory_space=pltpu.VMEM),
            pl.BlockSpec(memory_space=pltpu.VMEM),
            pl.BlockSpec(memory_space=pltpu.VMEM),
        ],
        out_specs=pl.BlockSpec((r, mz), row),
        compiler_params=pltpu.CompilerParams(vmem_limit_bytes=40 * 2**20),
        name="solve_z",
    )(t, low, high, lxy, lz, w1, w2)


def backward_kernel(kx, ky, mx, my, left, right, c3, ex, ey, out, *tmp):
    u = (left.at[0], right.at[0])

    @pl.loop(0, ky, unroll=8)
    def _(q):
        part = dot(ex[...], stack3(load_rows(u, q, kx, ky)))
        store_rows(tmp, q * mx, mx, part)

    @pl.loop(0, mx, unroll=8)
    def _(a):
        slab = stack3(load_rows(tmp, a, ky, mx))
        slab = jnp.concatenate([slab, c3[0, a]], axis=0)
        out[0, pl.ds(pl.multiple_of(a * my, 8), my), :] = dot(ey[...], slab)


def backward_xy(u, c3, ex3, ey3, kx, ky, mx, my):
    nv, rows, mz = u.shape
    wide = 2 * LANES
    return pl.pallas_call(
        functools.partial(backward_kernel, kx, ky, mx, my),
        grid=(nv, mz // wide),
        out_shape=jax.ShapeDtypeStruct((nv, mx * my, mz), F32),
        in_specs=[
            pl.BlockSpec((1, rows, LANES), lambda v, z: (v, 0, 2 * z)),
            pl.BlockSpec((1, rows, LANES), lambda v, z: (v, 0, 2 * z + 1)),
            pl.BlockSpec((1,) + c3.shape[1:3] + (wide,), lambda v, z: (v, 0, 0, z)),
            pl.BlockSpec(memory_space=pltpu.VMEM),
            pl.BlockSpec(memory_space=pltpu.VMEM),
        ],
        out_specs=pl.BlockSpec((1, mx * my, wide), lambda v, z: (v, 0, z)),
        scratch_shapes=[pltpu.VMEM((ky * mx, LANES), F32)] * 2,
        compiler_params=pltpu.CompilerParams(vmem_limit_bytes=32 * 2**20),
        name="backward_xy",
    )(u, u, c3, ex3, ey3)


def left3(m):
    hi, lo = split_host(m)
    return jnp.concatenate([hi, hi, lo], axis=1)


def shifted(x, axis, step):
    count = lax.axis_size(axis)
    pairs = [(i, i + step) for i in range(count) if 0 <= i + step < count]
    return lax.ppermute(x, axis, pairs)


def body(
    residual, eig_x, eig_y, eig_z, lam_x, lam_y, lam_z, basis_x, basis_y, basis_z, coarse_inverse
):
    w = NODES
    nv, mx, my, mz = residual.shape
    kx, ky, kz = eig_x.shape[1], eig_y.shape[1], eig_z.shape[1]
    funcs = basis_x.shape[1]
    bx, by, bz = basis_x[0], basis_y[0], basis_z[0]

    block = funcs**3
    bh, bl = split_host(jnp.tile(bz.T, (1, nv * funcs * funcs)))
    kron = (bx[:, None, :, None] * by[None, :, None, :]).reshape(funcs * funcs, mx * my)
    ext, every = extend(residual, jnp.concatenate([bh, bl], axis=1), left3(kron))
    ext = ext.reshape(nv, kx * ky, mz)

    coarse = jnp.swapaxes(every.reshape(-1, nv, block), 1, 2).reshape(-1, nv)
    sol = jnp.dot(coarse_inverse, coarse, precision=HIGH).T.reshape(nv, funcs, funcs, funcs)
    wide = jnp.einsum("vpqs,pa->vaqs", sol, bx, precision=HIGH)
    wide = jnp.einsum("vaqs,sc->vaqc", wide, bz, precision=HIGH)
    hi, lo = split_host(wide)
    pad = -(3 * funcs) % 16
    c3 = jnp.concatenate([hi, lo, hi, jnp.zeros((nv, mx, pad, mz), BF)], axis=2)

    ex, ey, ez = eig_x[0], eig_y[0], eig_z[0]
    t = forward_xy(ext, left3(ex.T), left3(ey.T), kx, ky)
    edge = jnp.concatenate(
        [t[:, :, : LANES // 2], t[:, :, mz - LANES // 2 :]], axis=2).reshape(-1, LANES)
    low, high = shifted(edge, "gz", 1), shifted(edge, "gz", -1)

    extra = LANES - (kz - mz)
    eh, el = split_host(jnp.pad(ez, ((0, 0), (0, extra))))
    gap = jnp.zeros((LANES - 7 * w, mz + LANES), BF)
    top, end = slice(0, w), slice(kz - w, kz)
    w1 = jnp.concatenate(
        [eh[w : w + mz], eh[w : w + mz], el[w : w + mz],
         eh[end], eh[top], eh[end], el[top], el[end], gap, jnp.zeros((w, mz + LANES), BF), eh[top]], axis=0)
    bh, bl = split_host(ez[w : w + mz].T)
    gap = jnp.zeros((LANES - 3 * (kz - mz), mz), BF)
    w2 = jnp.concatenate([bh[:mz], bh[:mz], bl[:mz], bh[mz:], bh[mz:], bl[mz:], gap], axis=0)
    lxy = jnp.broadcast_to(
        (lam_x[0][:, None] + lam_y[0][None, :]).reshape(kx * ky, 1), (kx * ky, LANES))
    lz = jnp.pad(lam_z[0], (0, extra), constant_values=1.0)[None]
    u = solve_z(t.reshape(nv * kx * ky, mz), low, high, lxy, lz, w1, w2)

    bh, bl = split_host(by.T)
    ey3 = jnp.concatenate(
        [left3(ey[w : w + my]), bh, bh, bl, jnp.zeros((my, pad), BF)], axis=1)
    out = backward_xy(
        u.reshape(nv, kx * ky, mz), c3, left3(ex[w : w + mx]), ey3, kx, ky, mx, my)
    return out.reshape(nv, mx, my, mz)


def solution(mesh):
    in_specs = (
        P(None, "gx", "gy", "gz"),
        P("gx", None, None),
        P("gy", None, None),
        P("gz", None, None),
        P("gx", None),
        P("gy", None),
        P("gz", None),
        P("gx", None, None),
        P("gy", None, None),
        P("gz", None, None),
        P(("gx", "gy", "gz"), None),
    )
    out_specs = P(None, "gx", "gy", "gz")
    return jax.shard_map(body, mesh=mesh, in_specs=in_specs, out_specs=out_specs, check_vma=False)
```

profile of v0, /device:TPU:1, one launch (start us, length us, event | category | flops | bytes accessed | tf_op | source)
XLA Modules:
  0.0 153.2 jit_solution(5096014593894129473)
XLA Ops:
  0.0 0.8 broadcast_multiply_fusion
  0.8 0.1 mul.26
  1.0 0.7 tile.4
  1.7 0.1 tile.10
  1.8 0.1 copy.28
  2.0 0.0 copy-done.9
  2.0 0.1 copy.31
  2.1 0.0 copy-done.10
  2.1 0.1 copy.30
  2.2 0.0 copy-start.2
  2.3 2.2 %copy-done.2 = f32[2,32,32,512]{3,2,1,0:T(8,128)S(1)} copy-done((f32[2,32,32,512]{3,2,1,0:T(8,128)S(1)}, f32[2,32,32,512]{3,2,1,0:T(8,128)}, u32[]{:S(2)}) %copy-start.2) | copy-done | bytes 4194328
  4.4 50.8 %halo.1 = (f32[2,48,48,512]{3,2,1,0:T(8,128)S(1)}, f32[4,4,2,1,128]{4,3,2,1,0:T(1,128)S(1)}) custom-call(f32[2,32,32,512]{3,2,1,0:T(8,128)S(1)} %copy-done.2, bf16[512,256]{1,0:T(8,128)(2,1)S(1)} %pad_maximum_fusion.1.bz, bf16[16,3072]{1,0:T(8,128)(2,1)S(1)} %pad_maximum_fusion.2.kron), custom_call_target="tpu_custom_call" | custom-call | tf_op jit(solution)/shard_map/halo/pallas_call | solution.py:240
  55.2 0.1 pad_maximum_fusion.3
  55.3 15.5 %forward_xy.1 = f32[2,2304,512]{2,1,0:T(8,128)S(1)} custom-call(f32[2,2304,512]{2,1,0:T(8,128)S(1)} %bitcast.70, f32[2,2304,512]{2,1,0:T(8,128)S(1)} %bitcast.71, bf16[48,144]{1,0:T(8,128)(2,1)S(1)} %get-tuple-element.31.ex, bf16[48,144]{1,0:T(8,128)(2,1)S(1)} %get-tuple-element.32.ey), custom_call_target="tpu_custom_call" | custom-call | tf_op jit(solution)/shard_map/forward_xy/pallas_call | solution.py:306
  70.8 0.0 copy-start.1
  70.8 0.9 fusion.26
  71.7 2.8 %copy-done.1 = f32[2,2304,512]{2,1,0:T(8,128)} copy-done((f32[2,2304,512]{2,1,0:T(8,128)}, f32[2,2304,512]{2,1,0:T(8,128)S(1)}, u32[]{:S(2)}) %copy-start.1) | copy-done | bytes 9437208
  74.5 2.1 %pad_maximum_fusion = f32[2,2304,128]{2,1,0:T(8,128)} fusion(f32[2,2304,64]{2,1,0:T(8,128)S(1)} %get-tuple-element.10, f32[2,2304,64]{2,1,0:T(8,128)S(1)} %get-tuple-element.9), kind=kLoop, calls=%fused_computation | loop fusion | flops 589824 | bytes 4718592 | tf_op jit(solution)/shard_map/concatenate | solution.py:436
  76.6 1.3 collective-permute-start
  77.9 6.6 %collective-permute-start.1 = (f32[4608,128]{1,0:T(8,128)}, f32[4608,128]{1,0:T(8,128)}, u32[]{:S(2)}, u32[]{:S(2)}) collective-permute-start(f32[4608,128]{1,0:T(8,128)} %bitcast.12), channel_id=1, source_target_pairs={{1,0},{3,2},{5,4},{7,6},{9,8},{11,10},{13,12},{15,14},{17,16},{19,... | collective-permute-start | bytes 7077896 | tf_op jit(solution)/shard_map/ppermute | solution.py:408
  84.4 0.0 copy-done.12
  84.4 0.1 copy.38
  84.5 0.0 copy-done.3
  84.6 1.1 slice.67
  85.7 0.2 fusion.1
  85.9 0.1 slice_dynamic-update-slice_fusion.1
  86.0 0.1 slice_dynamic-update-slice_fusion.2
  86.1 0.1 slice_dynamic-update-slice_fusion
  86.3 0.0 copy-start.15
  86.3 0.0 copy-start.16
  86.3 0.0 copy-start.14
  86.3 2.7 %copy.42 = f32[1,512,528]{1,2,0:T(8,128)} copy(f32[1,512,528]{2,1,0:T(8,128)} %slice.67) | data formatting | bytes 2162688
  89.0 2.2 %fusion.3 = (bf16[528,512]{1,0:T(8,128)(2,1)}, bf16[528,512]{1,0:T(8,128)(2,1)S(1)}) fusion(f32[1,512,528]{1,2,0:T(8,128)} %copy.42), kind=kLoop, calls=%fused_computation.9 | loop fusion | flops 1351680 | bytes 2162688 | tf_op jit(solution)/shard_map/convert_element_type | solution.py:19
  91.2 0.0 copy-done.15
  91.2 0.0 copy-done.16
  91.2 0.1 broadcast_add_fusion
  91.3 0.1 add.33
  91.4 0.0 copy-done.14
  91.4 0.5 broadcast.19
  91.9 0.6 reduce.4
  92.5 0.1 reshape.56
  92.6 0.1 reshape.59
  92.7 2.0 %dot_general.11 = f32[4,4,4,2048]{3,2,1,0:T(4,128)} reshape(f32[64,2048]{1,0:T(8,128)} %param.21) | data formatting | bytes 1048576 | tf_op jit(solution)/shard_map/dot_general | solution.py:427
  94.7 8.0 %fusion.20 = f32[2,4,4,4]{3,0,2,1:T(2,128)S(1)} fusion(f32[4,4,4,2048]{3,2,1,0:T(4,128)} %dot_general.11, f32[2048,2,1,1]{0,1,2,3:T(2,128)S(1)} %reshape.59), kind=kOutput, calls=%fused_computation.68 | convolution fusion | flops 3145728 | bytes 541184 | tf_op jit(solution)/shard_map/dot_general | solution.py:427
  102.8 0.0 copy-done.13
  102.8 0.3 convolution_bitcast_fusion
  103.0 1.5 fusion.27
  104.5 1.0 copy.53
  105.5 0.1 pad.16.clone
  105.6 0.1 pad_maximum_fusion.5.ex
  105.7 0.0 copy-done.4
  105.7 0.1 concatenate.39.ey
  106.0 0.9 copy-done.6
  107.0 0.1 copy-done.5
  107.0 0.2 copy-done.7
  107.2 0.6 fusion.5
  107.8 0.0 copy-done.8
  107.8 0.6 maximum_maximum_fusion.c3
  108.4 0.0 collective-permute-done.low
  108.5 0.0 collective-permute-done.1.high
  108.5 0.4 broadcast_in_dim.23.lxy
  108.8 26.2 %solve_z.1 = f32[4608,512]{1,0:T(8,128)} custom-call(f32[4608,512]{1,0:T(8,128)} %bitcast.69, f32[4608,128]{1,0:T(8,128)} %collective-permute-done.low, f32[4608,128]{1,0:T(8,128)} %collective-permute-done.1.high, f32[2304,128]{1,0:T(8,128)S(1)} %broadcast_in_dim.23.lxy, f32[1,640]{1,0:T(1,128)S(1)} %broadcast_in_dim.24.lz, ...), custom_call_target="tpu_custom_call" | custom-call | tf_op jit(solution)/shard_map/solve_z/pallas_call | solution.py:345
  135.1 3.7 %copy-done = f32[4608,512]{1,0:T(8,128)S(1)} copy-done((f32[4608,512]{1,0:T(8,128)S(1)}, f32[4608,512]{1,0:T(8,128)}, u32[]{:S(2)}) %copy-start) | copy-done | bytes 9437208
  138.7 14.5 %backward_xy.1 = f32[2,1024,512]{2,1,0:T(8,128)} custom-call(f32[2,2304,512]{2,1,0:T(8,128)S(1)} %bitcast.67, f32[2,2304,512]{2,1,0:T(8,128)S(1)} %bitcast.68, bf16[2,32,16,512]{3,2,1,0:T(8,128)(2,1)S(1)} %maximum_maximum_fusion.c3, bf16[32,144]{1,0:T(8,128)(2,1)S(1)} %pad_maximum_fusion.5.ex, bf16[32,160]{1,0:T(8,128)(2,1)S(1)} %concatenate.39.ey), custom_call_target="tpu_custom_call" | custom-call | tf_op jit(solution)/shard_map/backward_xy/pallas_call | solution.py:382
  (43 shorter events, 0.4 us)
Async XLA Ops:
  0.0 2.0 %copy-start.9 = (f32[1,48,48]{2,1,0:T(8,128)S(1)}, f32[1,48,48]{2,1,0:T(8,128)}, u32[]{:S(2)}) copy-start(f32[1,48,48]{2,1,0:T(8,128)} %param.13) | copy-start | bytes 27652
  0.0 2.1 %copy-start.10 = (f32[1,48,48]{2,1,0:T(8,128)S(1)}, f32[1,48,48]{2,1,0:T(8,128)}, u32[]{:S(2)}) copy-start(f32[1,48,48]{2,1,0:T(8,128)} %param.12) | copy-start | bytes 27652
  2.2 2.2 %copy-start.2 = (f32[2,32,32,512]{3,2,1,0:T(8,128)S(1)}, f32[2,32,32,512]{3,2,1,0:T(8,128)}, u32[]{:S(2)}) copy-start(f32[2,32,32,512]{3,2,1,0:T(8,128)} %res.1) | copy-start | bytes 12582916
  70.8 3.7 %copy-start.1 = (f32[2,2304,512]{2,1,0:T(8,128)}, f32[2,2304,512]{2,1,0:T(8,128)S(1)}, u32[]{:S(2)}) copy-start(f32[2,2304,512]{2,1,0:T(8,128)S(1)} %forward_xy.1) | copy-start | bytes 28311556
  74.5 9.9 %copy-start.12 = (f32[1,4,32]{2,1,0:T(4,128)S(1)}, f32[1,4,32]{2,1,0:T(4,128)}, u32[]{:S(2)}) copy-start(f32[1,4,32]{2,1,0:T(4,128)} %param.19) | copy-start | bytes 1540
  74.5 10.0 %copy-start.3 = (f32[1,528,528]{2,1,0:T(8,128)S(1)}, f32[1,528,528]{2,1,0:T(8,128)}, u32[]{:S(2)}) copy-start(f32[1,528,528]{2,1,0:T(8,128)} %param.14) | copy-start | bytes 3345412
  76.6 31.9 %collective-permute-start = (f32[4608,128]{1,0:T(8,128)}, f32[4608,128]{1,0:T(8,128)}, u32[]{:S(2)}, u32[]{:S(2)}) collective-permute-start(f32[4608,128]{1,0:T(8,128)} %bitcast.12), channel_id=1, source_target_pairs={{0,1},{2,3},{4,5},{6,7},{8,9},{10,11},{12,13},{14,15},{16,17},{18,... | collective-permute-start | bytes 7077896 | tf_op jit(solution)/shard_map/ppermute | solution.py:408
  77.9 30.6 %collective-permute-start.1 = (f32[4608,128]{1,0:T(8,128)}, f32[4608,128]{1,0:T(8,128)}, u32[]{:S(2)}, u32[]{:S(2)}) collective-permute-start(f32[4608,128]{1,0:T(8,128)} %bitcast.12), channel_id=1, source_target_pairs={{1,0},{3,2},{5,4},{7,6},{9,8},{11,10},{13,12},{15,14},{17,16},{19,... | collective-permute-start | bytes 7077896 | tf_op jit(solution)/shard_map/ppermute | solution.py:408
  86.3 5.0 %copy-start.15 = (f32[1,48]{1,0:T(1,128)S(1)}, f32[1,48]{1,0:T(1,128)}, u32[]{:S(2)}) copy-start(f32[1,48]{1,0:T(1,128)} %param.16) | copy-start | bytes 580
  86.3 5.0 %copy-start.16 = (f32[1,48]{1,0:T(1,128)S(1)}, f32[1,48]{1,0:T(1,128)}, u32[]{:S(2)}) copy-start(f32[1,48]{1,0:T(1,128)} %param.15) | copy-start | bytes 580
  86.3 5.1 %copy-start.14 = (f32[1,528]{1,0:T(1,128)S(1)}, f32[1,528]{1,0:T(1,128)}, u32[]{:S(2)}) copy-start(f32[1,528]{1,0:T(1,128)} %param.17) | copy-start | bytes 6340
  89.0 13.8 %copy-start.13 = (f32[1,4,32]{2,1,0:T(4,128)S(1)}, f32[1,4,32]{2,1,0:T(4,128)}, u32[]{:S(2)}) copy-start(f32[1,4,32]{2,1,0:T(4,128)} %param.18) | copy-start | bytes 1540
  89.0 14.0 %copy-start.11 = (f32[1,4,512]{2,1,0:T(4,128)S(1)}, f32[1,4,512]{2,1,0:T(4,128)}, u32[]{:S(2)}) copy-start(f32[1,4,512]{2,1,0:T(4,128)} %param.20) | copy-start | bytes 24580
  104.5 1.2 copy-start.4
  105.8 1.1 copy-start.6
  105.8 1.2 copy-start.5
  105.8 1.3 copy-start.7
  105.9 1.9 %copy-start.8 = (bf16[2,32,4,512]{3,2,1,0:T(4,128)(2,1)S(1)}, bf16[2,32,4,512]{3,2,1,0:T(4,128)(2,1)}, u32[]{:S(2)}) copy-start(bf16[2,32,4,512]{3,2,1,0:T(4,128)(2,1)} %copy.53) | copy-start | bytes 786436
  135.1 3.7 %copy-start = (f32[4608,512]{1,0:T(8,128)S(1)}, f32[4608,512]{1,0:T(8,128)}, u32[]{:S(2)}) copy-start(f32[4608,512]{1,0:T(8,128)} %solve_z.1) | copy-start | bytes 28311556
where the time goes:
time: 154 us; the launch traced here: 153 us
  Pallas kernels  107 us (69%)
  local copies, waits for them, and re-layouts  20.7 us (13%)
  matrix products  9.73 us (6%)
  starting transfers between devices  7.84 us (5%)
  other arithmetic  7.55 us (5%)
    pallas_call x1, Pallas kernels, extend(): pl.pallas_call(functools.partial(halo_kernel, sizes), out_shape=(jax.Shap...  50.8 us
    pallas_call x1, Pallas kernels, solve_z(): pl.pallas_call(functools.partial(z_kernel, mz), grid=(rows // r,), out_sh...  26.2 us
    pallas_call x1, Pallas kernels, forward_xy(): pl.pallas_call(functools.partial(forward_kernel, kx, ky), grid=(nv, mz //...  15.5 us
    pallas_call x1, Pallas kernels, backward_xy(): pl.pallas_call(functools.partial(backward_kernel, kx, ky, mx, my), grid=(...  14.5 us
    unnamed x53, local copies, waits for them, and re-layouts  13.1 us
    dot_general x1, matrix products, body(): jnp.dot(coarse_inverse, coarse, precision=HIGH)  8.02 us
    ppermute x2, starting transfers between devices, shifted(): return lax.ppermute(x, axis, pairs)  7.84 us
    convert_element_type x10, other arithmetic, split_host(): return (hi.astype(BF), lax.reduce_precision(x - hi, 8, 7).astype(BF))  3.13 us
  transfers between devices with their start and end apart: 2, of which 0 were waited for; matrix products, arithmetic and copies ran while one was open for 15% of the time, Pallas kernels for 0%

commit v1 on v0

--- a/solution.py
+++ b/solution.py
@@ -116,6 +116,11 @@
             def _():
                 send_x(side, c).start()
 
+    for side in range(2):
+        @pl.when(has_y[side])
+        def _():
+            send_y(side).start()
+
     own = pltpu.make_async_copy(
         res, ext.at[:, pl.ds(w, own_x), pl.ds(w, own_y)], own_sem
     )
@@ -171,14 +176,6 @@
     arrived(0)
     for copy in stage(1):
         copy.start()
-    for side in range(2):
-        @pl.when(has_y[side])
-        def _():
-            send_y(side).start()
-    arrived(1)
-    for copy in stage(2):
-        copy.start()
-
     def zero_x(side):
         return pltpu.make_async_copy(
             zeros.at[:, pl.ds(0, w)],
@@ -210,6 +207,9 @@
             @pl.when(both(a, c))
             def _():
                 send_c(a, c).start()
+    arrived(1)
+    for copy in stage(2):
+        copy.start()
     for a in range(2):
         pl.when(has_x[a])(lambda: get_x(a, 2).wait_recv())
         pl.when(has_y[a])(lambda: get_y(a).wait_recv())
@@ -263,7 +263,7 @@
             pltpu.SemaphoreType.DMA((3, peers)),
         ],
         compiler_params=pltpu.CompilerParams(
-            collective_id=0, has_side_effects=True, vmem_limit_bytes=32 * 2**20),
+            collective_id=0, has_side_effects=True, vmem_limit_bytes=56 * 2**20),
         name="halo",
     )(residual, bz, kron)
 
@@ -286,7 +286,7 @@
         ref[pl.ds(pl.multiple_of(start, 8), size), :] = value[:, i * LANES : (i + 1) * LANES]
 
 
-def forward_kernel(kx, ky, left, right, ex, ey, out, *tmp):
+def forward_kernel(kx, ky, left, right, ex, ey, out, edge, *tmp):
     ext = (left.at[0], right.at[0])
 
     @pl.loop(0, ky, unroll=8)
@@ -298,6 +298,15 @@
     def _(p):
         part = dot(ey[...], stack3(load_rows(tmp, p, ky, kx)))
         out[0, pl.ds(pl.multiple_of(p * ky, 8), ky), :] = part
+
+    @pl.when(pl.program_id(1) == 0)
+    def _():
+        edge[0] = out[0, :, :LANES]
+
+    @pl.when(pl.program_id(1) == pl.num_programs(1) - 1)
+    def _():
+        lane = lax.broadcasted_iota(jnp.int32, edge.shape[1:], 1)
+        edge[0] = jnp.where(lane < LANES // 2, edge[0], out[0, :, LANES:])
 
 
 def forward_xy(ext, ex3, ey3, kx, ky):
@@ -306,16 +315,22 @@
     return pl.pallas_call(
         functools.partial(forward_kernel, kx, ky),
         grid=(nv, mz // wide),
-        out_shape=jax.ShapeDtypeStruct(ext.shape, F32),
+        out_shape=(
+            jax.ShapeDtypeStruct(ext.shape, F32),
+            jax.ShapeDtypeStruct((nv, rows, LANES), F32),
+        ),
         in_specs=[
             pl.BlockSpec((1, rows, LANES), lambda v, z: (v, 0, 2 * z)),
             pl.BlockSpec((1, rows, LANES), lambda v, z: (v, 0, 2 * z + 1)),
             pl.BlockSpec(memory_space=pltpu.VMEM),
             pl.BlockSpec(memory_space=pltpu.VMEM),
         ],
-        out_specs=pl.BlockSpec((1, rows, wide), lambda v, z: (v, 0, z)),
+        out_specs=(
+            pl.BlockSpec((1, rows, wide), lambda v, z: (v, 0, z)),
+            pl.BlockSpec((1, rows, LANES), lambda v, z: (v, 0, 0)),
+        ),
         scratch_shapes=[pltpu.VMEM((rows, LANES), F32)] * 2,
-        compiler_params=pltpu.CompilerParams(vmem_limit_bytes=32 * 2**20),
+        compiler_params=pltpu.CompilerParams(vmem_limit_bytes=56 * 2**20),
         name="forward_xy",
     )(ext, ext, ex3, ey3)
 
@@ -356,7 +371,7 @@
             pl.BlockSpec(memory_space=pltpu.VMEM),
         ],
         out_specs=pl.BlockSpec((r, mz), row),
-        compiler_params=pltpu.CompilerParams(vmem_limit_bytes=40 * 2**20),
+        compiler_params=pltpu.CompilerParams(vmem_limit_bytes=56 * 2**20),
         name="solve_z",
     )(t, low, high, lxy, lz, w1, w2)
 
@@ -392,7 +407,7 @@
         ],
         out_specs=pl.BlockSpec((1, mx * my, wide), lambda v, z: (v, 0, z)),
         scratch_shapes=[pltpu.VMEM((ky * mx, LANES), F32)] * 2,
-        compiler_params=pltpu.CompilerParams(vmem_limit_bytes=32 * 2**20),
+        compiler_params=pltpu.CompilerParams(vmem_limit_bytes=56 * 2**20),
         name="backward_xy",
     )(u, u, c3, ex3, ey3)
 
@@ -424,7 +439,8 @@
     ext = ext.reshape(nv, kx * ky, mz)
 
     coarse = jnp.swapaxes(every.reshape(-1, nv, block), 1, 2).reshape(-1, nv)
-    sol = jnp.dot(coarse_inverse, coarse, precision=HIGH).T.reshape(nv, funcs, funcs, funcs)
+    coarse = lax.optimization_barrier(coarse)
+    sol = lax.optimization_barrier(jnp.dot(coarse_inverse, coarse, precision=HIGH)).T.reshape(nv, funcs, funcs, funcs)
     wide = jnp.einsum("vpqs,pa->vaqs", sol, bx, precision=HIGH)
     wide = jnp.einsum("vaqs,sc->vaqc", wide, bz, precision=HIGH)
     hi, lo = split_host(wide)
@@ -432,9 +448,8 @@
     c3 = jnp.concatenate([hi, lo, hi, jnp.zeros((nv, mx, pad, mz), BF)], axis=2)
 
     ex, ey, ez = eig_x[0], eig_y[0], eig_z[0]
-    t = forward_xy(ext, left3(ex.T), left3(ey.T), kx, ky)
-    edge = jnp.concatenate(
-        [t[:, :, : LANES // 2], t[:, :, mz - LANES // 2 :]], axis=2).reshape(-1, LANES)
+    t, edge = forward_xy(ext, left3(ex.T), left3(ey.T), kx, ky)
+    edge = edge.reshape(-1, LANES)
     low, high = shifted(edge, "gz", 1), shifted(edge, "gz", -1)
 
     extra = LANES - (kz - mz)

time: 154 us -> 149 us (0.968)
  matrix products: 9.73 us -> 1.39 us
  Pallas kernels: 107 us -> 114 us
  local copies, waits for them, and re-layouts: 20.7 us -> 16.4 us
    dot_general x1, matrix products: 8.02 us -> 0.51 us  [body(): jnp.dot(coarse_inverse, coarse, precision=HIGH)]
    unnamed x53 -> x47, local copies, waits for them, and re-layouts: 13.1 us -> 8.69 us
    pallas_call x1, Pallas kernels: 50.8 us -> 53.6 us  [extend(): pl.pallas_call(functools.partial(halo_kernel, sizes), out_shape=(jax.Shap...]
    concatenate x1 -> x0, other arithmetic: 2.08 us -> none  [body(): jnp.concatenate([t[:, :, :LANES // 2], t[:, :, mz - LANES // 2:]], axis=2)]
    pallas_call x1, Pallas kernels: 15.5 us -> 17.6 us  [forward_xy(): pl.pallas_call(functools.partial(forward_kernel, kx, ky), grid=(nv, mz //...]
    dot_general x1 -> x0, local copies, waits for them, and re-layouts: 2.01 us -> none  [body(): jnp.dot(coarse_inverse, coarse, precision=HIGH)]
    concatenate x3, other arithmetic: 0.19 us -> 2.04 us  [left3(): return jnp.concatenate([hi, hi, lo], axis=1)]
    pallas_call x1, Pallas kernels: 26.2 us -> 27.9 us  [solve_z(): pl.pallas_call(functools.partial(z_kernel, mz), grid=(rows // r,), out_sh...]
  transfers between devices with their start and end apart: 2 -> 2, of which waited for: 0 -> 0; matrix products, arithmetic and copies ran while one was open for 15% -> 14% of each run, Pallas kernels for 0% -> 0%
where the time goes in v1:
time: 149 us; the launch traced here: 148 us
  Pallas kernels  114 us (77%)
  local copies, waits for them, and re-layouts  16.4 us (11%)
  other arithmetic  8.19 us (5%)
  starting transfers between devices  7.85 us (5%)
    pallas_call x1, Pallas kernels, extend(): pl.pallas_call(functools.partial(halo_kernel, sizes), out_shape=(jax.Shap...  53.6 us
    pallas_call x1, Pallas kernels, solve_z(): pl.pallas_call(functools.partial(z_kernel, mz), grid=(rows // r,), out_sh...  27.9 us
    pallas_call x1, Pallas kernels, forward_xy(): pl.pallas_call(functools.partial(forward_kernel, kx, ky), grid=(nv, mz //...  17.6 us
    pallas_call x1, Pallas kernels, backward_xy(): pl.pallas_call(functools.partial(backward_kernel, kx, ky, mx, my), grid=(...  15.2 us
    unnamed x47, local copies, waits for them, and re-layouts  8.69 us
    ppermute x2, starting transfers between devices, shifted(): return lax.ppermute(x, axis, pairs)  7.85 us
  transfers between devices with their start and end apart: 2, of which 0 were waited for; matrix products, arithmetic and copies ran while one was open for 14% of the time, Pallas kernels for 0%

profile of v1, /device:TPU:1, one launch (start us, length us, event | category | flops | bytes accessed | tf_op | source)
XLA Modules:
  0.0 148.5 jit_solution(18245073598949187089)
XLA Ops:
  0.0 0.0 copy-start
  0.0 0.8 broadcast_multiply_fusion
  0.9 0.1 mul.26
  1.0 0.7 tile.4
  1.8 0.1 tile.10
  1.9 0.1 copy.28
  2.0 0.0 copy-done.5
  2.0 0.1 copy.31
  2.1 0.0 copy-done.6
  2.1 0.1 copy.30
  2.2 0.6 pad_maximum_fusion.1.kron
  2.9 0.7 pad_maximum_fusion.bz
  3.6 53.6 %halo.1 = (f32[2,48,48,512]{3,2,1,0:T(8,128)}, f32[4,4,2,1,128]{4,3,2,1,0:T(1,128)}) custom-call(f32[2,32,32,512]{3,2,1,0:T(8,128)} %res.1, bf16[512,256]{1,0:T(8,128)(2,1)} %pad_maximum_fusion.bz, bf16[16,3072]{1,0:T(8,128)(2,1)} %pad_maximum_fusion.1.kron), custom_call_target="tpu_custom_call" | custom-call | tf_op jit(solution)/shard_map/halo/pallas_call | solution.py:240
  57.3 0.7 pad_maximum_fusion.2
  58.0 17.6 %forward_xy.1 = (f32[2,2304,512]{2,1,0:T(8,128)}, f32[2,2304,128]{2,1,0:T(8,128)}) custom-call(f32[2,2304,512]{2,1,0:T(8,128)} %bitcast.70, f32[2,2304,512]{2,1,0:T(8,128)} %bitcast.71, bf16[48,144]{1,0:T(8,128)(2,1)} %get-tuple-element.33.ex, bf16[48,144]{1,0:T(8,128)(2,1)} %get-tuple-element.34.ey), custom_call_target="tpu_custom_call" | custom-call | tf_op jit(solution)/shard_map/forward_xy/pallas_call | solution.py:315
  75.5 1.3 collective-permute-start
  76.8 6.6 %collective-permute-start.1 = (f32[4608,128]{1,0:T(8,128)}, f32[4608,128]{1,0:T(8,128)}, u32[]{:S(2)}, u32[]{:S(2)}) collective-permute-start(f32[4608,128]{1,0:T(8,128)} %bitcast.83), channel_id=1, source_target_pairs={{1,0},{3,2},{5,4},{7,6},{9,8},{11,10},{13,12},{15,14},{17,16},{19,... | collective-permute-start | bytes 7077896 | tf_op jit(solution)/shard_map/ppermute | solution.py:423
  83.4 0.0 copy-done.9
  83.4 0.1 copy.38
  83.5 0.0 copy-done.1
  83.5 1.2 slice.59
  84.7 0.2 fusion.1
  84.9 0.0 copy-start.2
  84.9 0.9 slice_dynamic-update-slice_fusion.1
  85.8 0.9 slice_dynamic-update-slice_fusion.2
  86.7 0.9 slice_dynamic-update-slice_fusion
  87.6 0.6 constant_dynamic-update-slice_fusion.6
  88.2 0.6 constant_dynamic-update-slice_fusion.5
  88.8 0.6 constant_dynamic-update-slice_fusion.4
  89.4 0.6 constant_dynamic-update-slice_fusion.3
  90.0 0.6 constant_dynamic-update-slice_fusion.2
  90.6 0.7 broadcast_dynamic-update-slice_fusion
  91.3 0.0 copy-done.2
  91.3 0.0 copy-start.8
  91.3 0.0 copy-start.10
  91.3 0.0 copy-start.7
  91.3 1.4 copy.41
  92.7 1.4 fusion.3
  94.1 0.1 broadcast_add_fusion
  94.2 0.1 add.33
  94.3 0.6 broadcast_in_dim.24.lz
  94.9 0.5 broadcast.19
  95.4 0.6 reduce.4
  96.0 0.1 reshape.57
  96.1 0.1 reshape.58
  96.2 0.0 copy-done
  96.2 0.5 convolution_bitcast_fusion.1
  96.7 0.1 reshape.59
  96.9 0.0 copy-done.10
  96.9 0.2 convolution_bitcast_fusion
  97.1 0.6 fusion.24
  97.8 1.0 copy.52
  98.8 0.1 pad.16.clone
  98.9 0.7 pad_maximum_fusion.4.ex
  99.6 0.7 concatenate.35.ey
  100.3 0.6 constant_dynamic-update-slice_fusion.1
  101.1 0.6 constant_dynamic-update-slice_fusion.w1
  101.7 0.6 fusion.5
  102.3 1.6 %maximum_maximum_fusion.c3 = bf16[2,32,16,512]{3,2,1,0:T(8,128)(2,1)} fusion(bf16[2,32,4,512]{3,2,1,0:T(4,128)(2,1)S(1)} %copy-done.4, bf16[2,32,4,512]{3,2,1,0:T(4,128)(2,1)S(1)} %fusion.5, bf16[16]{0:T(256)(128)(2,1)S(1)} %pad.16.clone), kind=kLoop, calls=%fused_computation.10 | loop fusion | flops 4194304 | bytes 1572896 | tf_op jit(solution)/shard_map/concatenate | solution.py:448
  103.9 0.0 collective-permute-done.low
  103.9 0.0 collective-permute-done.1.high
  103.9 1.4 broadcast_in_dim.23.lxy
  105.3 27.9 %solve_z.1 = f32[4608,512]{1,0:T(8,128)} custom-call(f32[4608,512]{1,0:T(8,128)} %bitcast.72, f32[4608,128]{1,0:T(8,128)} %collective-permute-done.low, f32[4608,128]{1,0:T(8,128)} %collective-permute-done.1.high, f32[2304,128]{1,0:T(8,128)} %broadcast_in_dim.23.lxy, f32[1,640]{1,0:T(1,128)} %broadcast_in_dim.24.lz, ...), custom_call_target="tpu_custom_call" | custom-call | tf_op jit(solution)/shard_map/solve_z/pallas_call | solution.py:360
  133.2 15.2 %backward_xy.1 = f32[2,1024,512]{2,1,0:T(8,128)} custom-call(f32[2,2304,512]{2,1,0:T(8,128)} %bitcast.68, f32[2,2304,512]{2,1,0:T(8,128)} %bitcast.69, bf16[2,32,16,512]{3,2,1,0:T(8,128)(2,1)} %maximum_maximum_fusion.c3, bf16[32,144]{1,0:T(8,128)(2,1)} %pad_maximum_fusion.4.ex, bf16[32,160]{1,0:T(8,128)(2,1)} %concatenate.35.ey), custom_call_target="tpu_custom_call" | custom-call | tf_op jit(solution)/shard_map/backward_xy/pallas_call | solution.py:397
  (35 shorter events, 0.3 us)
Async XLA Ops:
  0.0 96.2 %copy-start = (f32[64,2048]{1,0:T(8,128)S(1)}, f32[64,2048]{1,0:T(8,128)}, u32[]{:S(2)}) copy-start(f32[64,2048]{1,0:T(8,128)} %param.21) | copy-start | bytes 1572868
  0.0 2.0 %copy-start.5 = (f32[1,48,48]{2,1,0:T(8,128)S(1)}, f32[1,48,48]{2,1,0:T(8,128)}, u32[]{:S(2)}) copy-start(f32[1,48,48]{2,1,0:T(8,128)} %param.13) | copy-start | bytes 27652
  0.0 2.1 %copy-start.6 = (f32[1,48,48]{2,1,0:T(8,128)S(1)}, f32[1,48,48]{2,1,0:T(8,128)}, u32[]{:S(2)}) copy-start(f32[1,48,48]{2,1,0:T(8,128)} %param.12) | copy-start | bytes 27652
  58.0 25.4 %copy-start.9 = (f32[1,4,32]{2,1,0:T(4,128)S(1)}, f32[1,4,32]{2,1,0:T(4,128)}, u32[]{:S(2)}) copy-start(f32[1,4,32]{2,1,0:T(4,128)} %param.19) | copy-start | bytes 1540
  58.0 25.5 %copy-start.1 = (f32[1,528,528]{2,1,0:T(8,128)S(1)}, f32[1,528,528]{2,1,0:T(8,128)}, u32[]{:S(2)}) copy-start(f32[1,528,528]{2,1,0:T(8,128)} %param.14) | copy-start | bytes 3345412
  75.5 28.4 %collective-permute-start = (f32[4608,128]{1,0:T(8,128)}, f32[4608,128]{1,0:T(8,128)}, u32[]{:S(2)}, u32[]{:S(2)}) collective-permute-start(f32[4608,128]{1,0:T(8,128)} %bitcast.82), channel_id=1, source_target_pairs={{0,1},{2,3},{4,5},{6,7},{8,9},{10,11},{12,13},{14,15},{16,17},{18,... | collective-permute-start | bytes 7077896 | tf_op jit(solution)/shard_map/ppermute | solution.py:423
  76.8 27.1 %collective-permute-start.1 = (f32[4608,128]{1,0:T(8,128)}, f32[4608,128]{1,0:T(8,128)}, u32[]{:S(2)}, u32[]{:S(2)}) collective-permute-start(f32[4608,128]{1,0:T(8,128)} %bitcast.83), channel_id=1, source_target_pairs={{1,0},{3,2},{5,4},{7,6},{9,8},{11,10},{13,12},{15,14},{17,16},{19,... | collective-permute-start | bytes 7077896 | tf_op jit(solution)/shard_map/ppermute | solution.py:423
  84.9 6.4 %copy-start.2 = (f32[1,512,528]{2,1,0:T(8,128)S(1)}, f32[1,512,528]{2,1,0:T(8,128)}, u32[]{:S(2)}) copy-start(f32[1,512,528]{2,1,0:T(8,128)} %slice.59) | copy-start | bytes 3244036
  91.3 2.8 %copy-start.12 = (f32[1,48]{1,0:T(1,128)S(1)}, f32[1,48]{1,0:T(1,128)}, u32[]{:S(2)}) copy-start(f32[1,48]{1,0:T(1,128)} %param.16) | copy-start | bytes 580
  91.3 2.8 %copy-start.13 = (f32[1,48]{1,0:T(1,128)S(1)}, f32[1,48]{1,0:T(1,128)}, u32[]{:S(2)}) copy-start(f32[1,48]{1,0:T(1,128)} %param.15) | copy-start | bytes 580
  91.3 3.0 %copy-start.11 = (f32[1,528]{1,0:T(1,128)S(1)}, f32[1,528]{1,0:T(1,128)}, u32[]{:S(2)}) copy-start(f32[1,528]{1,0:T(1,128)} %param.17) | copy-start | bytes 6340
  91.3 4.1 %copy-start.8 = (f32[4,4,2,1,128]{4,3,2,1,0:T(1,128)S(1)}, f32[4,4,2,1,128]{4,3,2,1,0:T(1,128)}, u32[]{:S(2)}) copy-start(f32[4,4,2,1,128]{4,3,2,1,0:T(1,128)} %get-tuple-element.12) | copy-start | bytes 49156
  91.3 5.6 %copy-start.10 = (f32[1,4,32]{2,1,0:T(4,128)S(1)}, f32[1,4,32]{2,1,0:T(4,128)}, u32[]{:S(2)}) copy-start(f32[1,4,32]{2,1,0:T(4,128)} %param.18) | copy-start | bytes 1540
  91.3 5.8 %copy-start.7 = (f32[1,4,512]{2,1,0:T(4,128)S(1)}, f32[1,4,512]{2,1,0:T(4,128)}, u32[]{:S(2)}) copy-start(f32[1,4,512]{2,1,0:T(4,128)} %param.20) | copy-start | bytes 24580
  100.9 1.4 copy-start.4
  101.1 4.3 %copy-start.3 = (bf16[1664,512]{1,0:T(8,128)(2,1)}, bf16[1664,512]{1,0:T(8,128)(2,1)S(1)}, u32[]{:S(2)}) copy-start(bf16[1664,512]{1,0:T(8,128)(2,1)S(1)} %broadcast_dynamic-update-slice_fusion.1.w2) | copy-start | bytes 5111812
